TPU v7x, 32 devices: a whole 2x2x4 slice. The times are simulated.
32 devices in a mesh: layer: 4 (over y, x), row: 2 (over core), col: 4 (over z).
Axes of the slice: x: 2, y: 2, z: 4, core: 2. Of those that a mesh axis runs over, the one named last changes fastest.
Arguments:
- hidden: bfloat16 [384, 2304], P(('layer', 'row')), may hold values from -60 to 60
- embedding: bfloat16 [16384, 2304], P(('row', 'col'), 'layer'), may hold values from -0.3 to 0.3
- teacher: bfloat16 [384, 16384], P('layer', ('row', 'col')), may hold values from -80 to 240
Outputs:
- grad_embedding: float32 [16384, 2304], P(('row', 'col'), 'layer')
- grad_hidden: float32 [384, 2304], P(('layer', 'row', 'col'))
All inputs are finite; a program needn't handle non-finite values.
Results may differ from a plain program's by a relative error of at most 0.0041.
Values may be sent and summed in bfloat16 or wider, within the bound.
A program may use at most 192 MiB of HBM per device.

v0:
```python
import jax
import jax.numpy as jnp
from jax import lax
from jax.sharding import PartitionSpec as P

LOSS_SCALE = 256


def local(hidden, embedding, teacher):
    token_rows = lax.all_gather(hidden, "row", axis=0, tiled=True)
    width_part = lax.all_to_all(token_rows, "layer", split_axis=1, concat_axis=0, tiled=True)
    logits = lax.psum_scatter(
        lax.dot_general(
            width_part, embedding, (((1,), (1,)), ((), ())), preferred_element_type=jnp.float32
        ),
        "layer",
        scatter_dimension=0,
        tiled=True,
    )
    teach_f = teacher.astype(jnp.float32)
    top_s, top_t = lax.pmax((jnp.max(logits, axis=1), jnp.max(teach_f, axis=1)), ("row", "col"))
    part_s = jnp.sum(jnp.exp(logits - top_s[:, None]), axis=1)
    part_t = jnp.sum(jnp.exp(teach_f - top_t[:, None]), axis=1)
    sum_s, sum_t = lax.psum((part_s, part_t), ("row", "col"))
    lse_s = top_s + jnp.log(sum_s)
    lse_t = top_t + jnp.log(sum_t)
    prob_s = jnp.exp(logits - lse_s[:, None])
    prob_t = jnp.exp(teach_f - lse_t[:, None])
    grads = ((prob_s - prob_t) * LOSS_SCALE).astype(jnp.bfloat16)
    grad_piece = lax.all_gather(grads, "layer", axis=0, tiled=True)
    embed_acc = lax.dot_general(
        grad_piece, width_part, (((0,), (0,)), ((), ())), preferred_element_type=jnp.float32
    )
    hidden_piece = jnp.dot(grad_piece, embedding, preferred_element_type=jnp.float32)
    hidden_terms = lax.all_to_all(hidden_piece, "layer", split_axis=0, concat_axis=1, tiled=True)
    grad_hidden = lax.psum_scatter(hidden_terms, ("row", "col"), scatter_dimension=0, tiled=True)
    return (embed_acc, grad_hidden)


def solution(mesh):
    placed = (P(("layer", "row"), None), P(("row", "col"), "layer"), P("layer", ("row", "col")))
    return jax.shard_map(
        local,
        mesh=mesh,
        in_specs=placed,
        out_specs=(P(("row", "col"), "layer"), P(("layer", "row", "col"), None)),
        check_vma=False,
    )
```

profile of v0, /device:TPU:1, one launch (start us, length us, event | category | flops | bytes accessed | tf_op | source)
XLA Modules:
  0.0 216.0 jit_solution(10763876937868347929)
XLA Ops:
  7.2 0.0 copy-start
  7.2 0.0 reduce-scatter.4.cloned.1.call-start
  7.2 2.5 %all_gather.6 = bf16[96,2304]{1,0:T(8,128)(2,1)S(1)} all-gather(bf16[48,2304]{1,0:T(8,128)(2,1)} %param.3), channel_id=1, replica_groups=mesh['layer'=4,'row'=2,'col'=4] {'row'}, dimensions={0}, use_global_device_ids=true | all-gather | bytes 663552 | tf_op jit(solution)/shard_map/all_gather | solution.py:10
  9.7 0.6 all_to_all.28
  10.3 0.1 copy.11
  10.3 11.5 %all_to_all.38 = bf16[96,4,576]{2,0,1:T(8,128)(2,1)S(1)} all-to-all(bf16[96,4,576]{2,0,1:T(8,128)(2,1)S(1)} %copy.11), channel_id=1, replica_groups=mesh['layer'=4,'row'=2,'col'=4] {'layer'}, dimensions={1} | all-to-all | bytes 884736 | tf_op jit(solution)/shard_map/all_to_all | solution.py:11
  21.8 0.0 copy-start.2
  21.8 0.8 copy-done.2
  22.6 0.0 copy-done
  22.6 3.1 %fusion.7 = f32[384,2048]{1,0:T(8,128)} fusion(bf16[384,576]{1,0:T(8,128)(2,1)S(1)} %bitcast.14, bf16[2048,576]{0,1:T(8,128)(2,1)S(1)} %copy-done), kind=kOutput, calls=%fused_computation.12 | convolution fusion | flops 905969664 | bytes 5947392 | tf_op jit(solution)/shard_map/dot_general | solution.py:13
  25.7 0.0 copy-start.5
  25.7 0.0 reduce-scatter.4.cloned.1.call-update
  25.7 0.0 all-gather.2.cloned.1.call-start
  25.8 0.9 copy-done.5
  26.7 0.2 reduce_max.24
  26.8 43.8 %reduce-scatter.4.cloned.1.call-done = f32[96,2048]{1,0:T(8,128)} async-done(((f32[384,2048]{1,0:T(8,128)}), f32[96,2048]{1,0:T(8,128)}) %reduce-scatter.4.cloned.1.call-update) | async-done | bytes 786448 | tf_op jit(solution)/shard_map/reduce_scatter | solution.py:12
  70.6 0.0 copy-start.1
  70.6 1.3 reduce_max.23
  72.0 17.8 %all-reduce.3 = (f32[96]{0:T(128)S(1)}, f32[96]{0:T(128)S(1)}) all-reduce(bf16[96]{0:T(256)(128)(2,1)S(1)} %reduce_max.24, f32[96]{0:T(128)S(1)} %reduce_max.23), channel_id=1, replica_groups=mesh['layer'=4,'row'=2,'col'=4] {'row','col'}, use_global_device_ids=true, to_apply=%region_6.0 | all-reduce | flops 192 | bytes 1344 | tf_op jit(solution)/shard_map/pmax | solution.py:21
  89.8 1.5 fusion.2
  91.4 14.2 %all-reduce.2 = (f32[96]{0:T(128)}, f32[96]{0:T(128)}) all-reduce(f32[96]{0:T(128)S(1)} %get-tuple-element.6, f32[96]{0:T(128)S(1)} %get-tuple-element.7), channel_id=1, replica_groups=mesh['layer'=4,'row'=2,'col'=4] {'row','col'}, use_global_device_ids=true, to_apply=%region_8.0 | all-reduce | flops 192 | bytes 1536 | tf_op jit(solution)/shard_map/psum | solution.py:24
  105.6 0.7 log_add_fusion
  106.2 0.7 log_add_fusion.1
  106.9 0.0 copy-done.1
  106.9 1.1 fusion.6
  108.0 0.0 all-gather.2.cloned.1.call-update
  108.0 0.0 copy-start.6
  108.0 29.8 %all-gather.2.cloned.1.call-done = bf16[384,2048]{1,0:T(8,128)(2,1)} async-done(((bf16[96,2048]{1,0:T(8,128)(2,1)}), bf16[384,2048]{1,0:T(8,128)(2,1)}) %all-gather.2.cloned.1.call-update) | async-done | bytes 1572880 | tf_op jit(solution)/shard_map/all_gather | solution.py:30
  137.8 3.8 %fusion.9 = f32[384,576]{1,0:T(8,128)} fusion(bf16[384,2048]{1,0:T(8,128)(2,1)} %all-gather.2.cloned.1.call-done, bf16[2048,576]{0,1:T(8,128)(2,1)S(1)} %copy-done), kind=kOutput, calls=%fused_computation.14 | convolution fusion | flops 905969664 | bytes 4816896 | tf_op jit(solution)/shard_map/dot_general | solution.py:34
  141.6 3.5 %all-to-all-start.1 = ((f32[4,96,576]{2,1,0:T(8,128)}), f32[4,96,576]{2,1,0:T(8,128)S(1)}, u32[]{:S(2)}, u32[]{:S(2)}) async-start(f32[4,96,576]{2,1,0:T(8,128)} %bitcast.17), calls=%async_computation.2 | async-start | bytes 1966080 | tf_op jit(solution)/shard_map/all_to_all | solution.py:35
  145.1 0.0 copy-done.6
  145.1 0.6 dynamic-slice.4
  146.3 11.2 %all-to-all-done.1 = f32[4,96,576]{2,1,0:T(8,128)S(1)} async-done(((f32[4,96,576]{2,1,0:T(8,128)}), f32[4,96,576]{2,1,0:T(8,128)S(1)}, u32[]{:S(2)}, u32[]{:S(2)}) %all-to-all-start.1) | async-done | bytes 884768 | tf_op jit(solution)/shard_map/all_to_all | solution.py:35
  157.5 0.0 copy-start.4
  157.5 0.9 copy-done.4
  158.4 0.0 copy-start.3
  158.4 2.8 %copy.13 = f32[96,4,576]{2,1,0:T(4,128)} copy(f32[96,4,576]{2,0,1:T(8,128)} %bitcast.16) | data formatting | bytes 1769472 | tf_op jit(solution)/shard_map/all_to_all | solution.py:35
  161.3 2.7 %all_to_all.35 = f32[96,2304]{1,0:T(8,128)} reshape(f32[96,4,576]{2,1,0:T(4,128)} %copy.13) | data formatting | bytes 1769472 | tf_op jit(solution)/shard_map/all_to_all | solution.py:35
  164.0 32.7 %fusion = f32[16,2304]{1,0:T(8,128)S(1)} fusion(f32[96,2304]{1,0:T(8,128)} %all_to_all.35), kind=kCustom, calls=%all-reduce-scatter | all-reduce-scatter fusion | flops 294913 | bytes 1032704
  196.7 1.9 collective-permute-start
  198.6 2.4 %collective-permute-start.1 = (f32[12,2304]{1,0:T(8,128)S(1)}, f32[12,2304]{1,0:T(8,128)S(1)}, u32[]{:S(2)}, u32[]{:S(2)}) collective-permute-start(f32[12,2304]{1,0:T(8,128)S(1)} %slice), channel_id=1, source_target_pairs={{0,2},{1,3},{2,4},{3,5},{4,6},{5,7},{8,10},{9,11},{10,12},{11,13},... | collective-permute-start | bytes 331784
  201.0 0.0 copy-done.3
  201.0 5.0 %fusion.8 = f32[2048,576]{0,1:T(8,128)} fusion(bf16[384,2048]{1,0:T(8,128)(2,1)} %all-gather.2.cloned.1.call-done, bf16[384,576]{1,0:T(8,128)(2,1)S(1)} %bitcast.15), kind=kOutput, calls=%fused_computation.13 | convolution fusion | flops 905969664 | bytes 6733824 | tf_op jit(solution)/shard_map/dot_general | solution.py:31
  206.1 2.0 collective-permute-done.1
  208.1 0.0 collective-permute-done
  208.1 0.4 concatenate
  208.5 0.7 constant_dynamic-slice_fusion
  (1 shorter events, 0.0 us)
Async XLA Ops:
  7.2 15.5 %copy-start = (bf16[2048,576]{0,1:T(8,128)(2,1)S(1)}, bf16[2048,576]{0,1:T(8,128)(2,1)}, u32[]{:S(2)}) copy-start(bf16[2048,576]{0,1:T(8,128)(2,1)} %param.4) | copy-start | bytes 7077892
  7.2 63.5 %reduce-scatter.4.cloned.1.call-start = ((), (), s32[]{:S(2)}) async-start(), calls=%async_computation.3 | async-start | bytes 3932160 | tf_op jit(solution)/shard_map/reduce_scatter | solution.py:12
  21.8 0.8 copy-start.2
  25.7 1.0 copy-start.5
  25.7 112.1 %all-gather.2.cloned.1.call-start = ((), (), s32[]{:S(2)}) async-start(), calls=%async_computation.4 | async-start | bytes 1966080 | tf_op jit(solution)/shard_map/all_gather | solution.py:30
  70.6 36.2 %copy-start.1 = (f32[96,2048]{1,0:T(8,128)S(1)}, f32[96,2048]{1,0:T(8,128)}, u32[]{:S(2)}) copy-start(f32[96,2048]{1,0:T(8,128)} %reduce-scatter.4.cloned.1.call-done) | copy-start | bytes 2359300
  108.0 37.1 %copy-start.6 = (u32[32]{0:T(128)S(1)}, u32[32]{0:T(128)}, u32[]{:S(2)}) copy-start(u32[32]{0:T(128)} %constant.10) | copy-start | bytes 388
  141.6 15.9 %all-to-all-start.1 = ((f32[4,96,576]{2,1,0:T(8,128)}), f32[4,96,576]{2,1,0:T(8,128)S(1)}, u32[]{:S(2)}, u32[]{:S(2)}) async-start(f32[4,96,576]{2,1,0:T(8,128)} %bitcast.17), calls=%async_computation.2 | async-start | bytes 1966080 | tf_op jit(solution)/shard_map/all_to_all | solution.py:35
  157.5 0.9 copy-start.4
  158.4 42.6 %copy-start.3 = (bf16[96,4,576]{2,0,1:T(8,128)(2,1)S(1)}, bf16[96,4,576]{2,0,1:T(8,128)(2,1)}, u32[]{:S(2)}) copy-start(bf16[96,4,576]{2,0,1:T(8,128)(2,1)} %copy-done.2) | copy-start | bytes 1327108
  196.7 11.4 %collective-permute-start = (f32[16,2304]{1,0:T(8,128)S(1)}, f32[16,2304]{1,0:T(8,128)S(1)}, u32[]{:S(2)}, u32[]{:S(2)}) collective-permute-start(f32[16,2304]{1,0:T(8,128)S(1)} %fusion), channel_id=1, source_target_pairs={{0,1},{1,2},{2,3},{3,4},{4,5},{5,6},{6,7},{8,9},{9,10},{10,11},{11... | collective-permute-start | bytes 442376
  198.6 9.5 %collective-permute-start.1 = (f32[12,2304]{1,0:T(8,128)S(1)}, f32[12,2304]{1,0:T(8,128)S(1)}, u32[]{:S(2)}, u32[]{:S(2)}) collective-permute-start(f32[12,2304]{1,0:T(8,128)S(1)} %slice), channel_id=1, source_target_pairs={{0,2},{1,3},{2,4},{3,5},{4,6},{5,7},{8,10},{9,11},{10,12},{11,13},... | collective-permute-start | bytes 331784
Sparse Core Ops, SparseCore 0:
  25.8 44.7 reduce-scatter.3
  108.1 29.6 all-gather.1
where the time goes:
time: 217 us; the launch traced here: 216 us
  waiting for transfers between devices  86.8 us (40%)
  blocking collectives  78.7 us (36%)
  between operations  14.8 us (7%)
  matrix products  11.9 us (5%)
  local copies, waits for them, and re-layouts  10.5 us (5%)
  starting transfers between devices  7.91 us (4%)
  other arithmetic  5.41 us (2%)
    reduce_scatter x1, waiting for transfers between devices, local(): lax.psum_scatter(lax.dot_general(width_part, embedding, (((1,), (1,)), ((...  43.8 us
    unnamed x1, blocking collectives  32.7 us
    all_gather x1, waiting for transfers between devices, local(): grad_piece = lax.all_gather(grads, 'layer', axis=0, tiled=True)  29.8 us
    pmax x1, blocking collectives, local(): lax.pmax((jnp.max(logits, axis=1), jnp.max(teach_f, axis=1)), ('row', 'co...  17.8 us
    psum x1, blocking collectives, local(): sum_s, sum_t = lax.psum((part_s, part_t), ('row', 'col'))  14.2 us
    all_to_all x1, blocking collectives, local(): lax.all_to_all(token_rows, 'layer', split_axis=1, concat_axis=0, tiled=True)  11.5 us
    all_to_all x1, waiting for transfers between devices, local(): lax.all_to_all(hidden_piece, 'layer', split_axis=0, concat_axis=1, tiled=...  11.2 us
    all_to_all x2, local copies, waits for them, and re-layouts, local(): lax.all_to_all(hidden_piece, 'layer', split_axis=0, concat_axis=1, tiled=...  5.53 us
  transfers between devices with their start and end apart: 5, of which 4 were waited for; matrix products, arithmetic and copies ran while one was open for 3% of the time, Pallas kernels for 0%

commit v1 on v0

--- a/solution.py
+++ b/solution.py
@@ -27,7 +27,22 @@
     prob_s = jnp.exp(logits - lse_s[:, None])
     prob_t = jnp.exp(teach_f - lse_t[:, None])
     grads = ((prob_s - prob_t) * LOSS_SCALE).astype(jnp.bfloat16)
-    grad_piece = lax.all_gather(grads, "layer", axis=0, tiled=True)
+
+    def draw_the_turns(q_in):
+        n_shards = lax.axis_size("layer")
+        trail = tuple(((p, (p + 1) % n_shards) for p in range(n_shards)))
+
+        def pass_the_routes_all(step_out):
+            if len(step_out) == n_shards:
+                return step_out
+            raw_out = lax.ppermute(step_out[0], "layer", trail)
+            return pass_the_routes_all([raw_out, *step_out])
+
+        b_next = pass_the_routes_all([q_in])
+        kept_arr = jnp.concatenate(b_next, axis=0)
+        return jnp.roll(kept_arr, (lax.axis_index("layer") + 1) * q_in.shape[0], axis=0)
+
+    grad_piece = draw_the_turns(grads)
     embed_acc = lax.dot_general(
         grad_piece, width_part, (((0,), (0,)), ((), ())), preferred_element_type=jnp.float32
     )

time: 217 us -> 221 us (1.018)
  waiting for transfers between devices: 86.8 us -> 90.7 us
  local copies, waits for them, and re-layouts: 10.5 us -> 13.8 us
  blocking collectives: 78.7 us -> 76.2 us
    ppermute x0 -> x3, waiting for transfers between devices: none -> 32.1 us  [pass_the_routes_all(): raw_out = lax.ppermute(step_out[0], 'layer', trail)]
    all_gather x1 -> x0, waiting for transfers between devices: 29.8 us -> none  [local(): grad_piece = lax.all_gather(grads, 'layer', axis=0, tiled=True)]
    unnamed x18 -> x23, local copies, waits for them, and re-layouts: 4.34 us -> 7.61 us
  transfers between devices with their start and end apart: 5 -> 7, of which waited for: 4 -> 6; matrix products, arithmetic and copies ran while one was open for 3% -> 3% of each run, Pallas kernels for 0% -> 0%
where the time goes in v1:
time: 221 us; the launch traced here: 220 us
  waiting for transfers between devices  90.7 us (41%)
  blocking collectives  76.2 us (34%)
  between operations  14.9 us (7%)
  local copies, waits for them, and re-layouts  13.8 us (6%)
  matrix products  10.5 us (5%)
  starting transfers between devices  9.63 us (4%)
  other arithmetic  4.54 us (2%)
    reduce_scatter x1, waiting for transfers between devices, local(): lax.psum_scatter(lax.dot_general(width_part, embedding, (((1,), (1,)), ((...  44.8 us
    ppermute x3, waiting for transfers between devices, pass_the_routes_all(): raw_out = lax.ppermute(step_out[0], 'layer', trail)  32.1 us
    unnamed x1, blocking collectives  30.7 us
    pmax x1, blocking collectives, local(): lax.pmax((jnp.max(logits, axis=1), jnp.max(teach_f, axis=1)), ('row', 'co...  17.8 us
    psum x1, blocking collectives, local(): sum_s, sum_t = lax.psum((part_s, part_t), ('row', 'col'))  13.7 us
    all_to_all x1, blocking collectives, local(): lax.all_to_all(token_rows, 'layer', split_axis=1, concat_axis=0, tiled=True)  11.5 us
    all_to_all x1, waiting for transfers between devices, local(): lax.all_to_all(hidden_piece, 'layer', split_axis=0, concat_axis=1, tiled=...  11.3 us
    unnamed x23, local copies, waits for them, and re-layouts  7.61 us
  transfers between devices with their start and end apart: 7, of which 6 were waited for; matrix products, arithmetic and copies ran while one was open for 3% of the time, Pallas kernels for 0%

profile of v1, /device:TPU:1, one launch (start us, length us, event | category | flops | bytes accessed | tf_op | source)
XLA Modules:
  0.0 220.2 jit_solution(13972123578201793514)
XLA Ops:
  7.2 0.0 copy-start
  7.2 0.0 reduce-scatter.4.cloned.1.call-start
  7.2 2.5 %all_gather.3 = bf16[96,2304]{1,0:T(8,128)(2,1)S(1)} all-gather(bf16[48,2304]{1,0:T(8,128)(2,1)} %param.3), channel_id=1, replica_groups=mesh['layer'=4,'row'=2,'col'=4] {'row'}, dimensions={0}, use_global_device_ids=true | all-gather | bytes 663552 | tf_op jit(solution)/shard_map/all_gather | solution.py:10
  9.7 0.6 all_to_all.28
  10.3 0.1 copy.11
  10.3 11.5 %all_to_all.38 = bf16[96,4,576]{2,0,1:T(8,128)(2,1)S(1)} all-to-all(bf16[96,4,576]{2,0,1:T(8,128)(2,1)S(1)} %copy.11), channel_id=1, replica_groups=mesh['layer'=4,'row'=2,'col'=4] {'layer'}, dimensions={1} | all-to-all | bytes 884736 | tf_op jit(solution)/shard_map/all_to_all | solution.py:11
  21.8 0.0 copy-done
  21.8 3.1 %fusion.13 = f32[384,2048]{1,0:T(8,128)} fusion(bf16[384,576]{1,0:T(8,128)(2,1)S(1)} %bitcast.12, bf16[2048,576]{0,1:T(8,128)(2,1)S(1)} %copy-done), kind=kOutput, calls=%fused_computation.26 | convolution fusion | flops 905969664 | bytes 5947392 | tf_op jit(solution)/shard_map/dot_general | solution.py:13
  24.9 0.0 reduce-scatter.4.cloned.1.call-update
  24.9 0.0 copy-done.1
  24.9 0.2 reduce_max.24
  25.1 44.8 %reduce-scatter.4.cloned.1.call-done = f32[96,2048]{1,0:T(8,128)} async-done(((f32[384,2048]{1,0:T(8,128)}), f32[96,2048]{1,0:T(8,128)}) %reduce-scatter.4.cloned.1.call-update) | async-done | bytes 786448 | tf_op jit(solution)/shard_map/reduce_scatter | solution.py:12
  69.8 1.3 reduce_max.23
  71.1 17.8 %all-reduce.3 = (f32[96]{0:T(128)S(1)}, f32[96]{0:T(128)S(1)}) all-reduce(bf16[96]{0:T(256)(128)(2,1)S(1)} %reduce_max.24, f32[96]{0:T(128)S(1)} %reduce_max.23), channel_id=1, replica_groups=mesh['layer'=4,'row'=2,'col'=4] {'row','col'}, use_global_device_ids=true, to_apply=%region_6.0 | all-reduce | flops 192 | bytes 1344 | tf_op jit(solution)/shard_map/pmax | solution.py:21
  88.9 1.5 fusion.6
  90.5 13.7 %all-reduce.2 = (f32[96]{0:T(128)S(1)}, f32[96]{0:T(128)S(1)}) all-reduce(f32[96]{0:T(128)S(1)} %get-tuple-element.6, f32[96]{0:T(128)S(1)} %get-tuple-element.7), channel_id=1, replica_groups=mesh['layer'=4,'row'=2,'col'=4] {'row','col'}, use_global_device_ids=true, to_apply=%region_8.0 | all-reduce | flops 192 | bytes 1536 | tf_op jit(solution)/shard_map/psum | solution.py:24
  104.2 1.6 fusion.10
  105.8 1.2 collective-permute-start
  107.0 10.7 %collective-permute-done = bf16[96,2048]{1,0:T(8,128)(2,1)S(1)} collective-permute-done((bf16[96,2048]{1,0:T(8,128)(2,1)S(1)}, bf16[96,2048]{1,0:T(8,128)(2,1)S(1)}, u32[]{:S(2)}, u32[]{:S(2)}) %collective-permute-start) | collective-permute-done | bytes 393248 | tf_op jit(solution)/shard_map/ppermute | solution.py:38
  117.7 0.7 copy-done.2
  118.5 0.3 collective-permute-start.1
  118.8 10.9 %collective-permute-done.1 = bf16[96,2048]{1,0:T(8,128)(2,1)} collective-permute-done((bf16[96,2048]{1,0:T(8,128)(2,1)S(1)}, bf16[96,2048]{1,0:T(8,128)(2,1)}, u32[]{:S(2)}, u32[]{:S(2)}) %collective-permute-start.1) | collective-permute-done | bytes 393248 | tf_op jit(solution)/shard_map/ppermute | solution.py:38
  129.6 0.0 collective-permute-start.2
  129.6 10.5 %collective-permute-done.2 = bf16[96,2048]{1,0:T(8,128)(2,1)} collective-permute-done((bf16[96,2048]{1,0:T(8,128)(2,1)}, bf16[96,2048]{1,0:T(8,128)(2,1)}, u32[]{:S(2)}, u32[]{:S(2)}) %collective-permute-start.2) | collective-permute-done | bytes 393248 | tf_op jit(solution)/shard_map/ppermute | solution.py:38
  140.2 1.0 constant_dynamic-update-slice_fusion.7
  141.2 1.0 constant_dynamic-update-slice_fusion.6
  142.2 1.0 constant_dynamic-update-slice_fusion.5
  143.3 1.0 constant_dynamic-update-slice_fusion.3
  144.3 1.0 constant_dynamic-update-slice_fusion.2
  145.3 0.0 copy-done.3
  145.4 0.0 copy-start.4
  145.4 0.0 copy-start.5
  145.4 2.4 %fusion.1 = f32[384,576]{1,0:T(8,128)} fusion(bf16[2048,576]{0,1:T(8,128)(2,1)S(1)} %copy-done, bf16[768,2048]{1,0:T(8,128)(2,1)S(1)} %constant_dynamic-update-slice_fusion, s32[]{:T(128)S(6)} %select_n.14), kind=kOutput, calls=%fused_computation | convolution fusion | flops 905969664 | bytes 4816900 | tf_op jit(solution)/shard_map/dot_general | solution.py:49
  147.8 0.0 copy-done.4
  147.8 4.2 %all-to-all-start.1 = ((f32[4,96,576]{2,1,0:T(8,128)}), f32[4,96,576]{2,1,0:T(8,128)}, u32[]{:S(2)}, u32[]{:S(2)}) async-start(f32[4,96,576]{2,1,0:T(8,128)} %bitcast.14), calls=%async_computation.2 | async-start | bytes 1966080 | tf_op jit(solution)/shard_map/all_to_all | solution.py:50
  152.1 0.0 copy-done.5
  152.1 0.6 dynamic-slice.4
  153.3 11.3 %all-to-all-done.1 = f32[4,96,576]{2,1,0:T(8,128)} async-done(((f32[4,96,576]{2,1,0:T(8,128)}), f32[4,96,576]{2,1,0:T(8,128)}, u32[]{:S(2)}, u32[]{:S(2)}) %all-to-all-start.1) | async-done | bytes 884768 | tf_op jit(solution)/shard_map/all_to_all | solution.py:50
  164.6 2.8 %copy.13 = f32[96,4,576]{2,1,0:T(4,128)} copy(f32[96,4,576]{2,0,1:T(8,128)} %bitcast.3) | data formatting | bytes 1769472 | tf_op jit(solution)/shard_map/all_to_all | solution.py:50
  167.3 2.7 %all_to_all.35 = f32[96,2304]{1,0:T(8,128)} reshape(f32[96,4,576]{2,1,0:T(4,128)} %copy.13) | data formatting | bytes 1769472 | tf_op jit(solution)/shard_map/all_to_all | solution.py:50
  170.1 30.7 %fusion = f32[16,2304]{1,0:T(8,128)S(1)} fusion(f32[96,2304]{1,0:T(8,128)} %all_to_all.35), kind=kCustom, calls=%all-reduce-scatter | all-reduce-scatter fusion | flops 294913 | bytes 1032704
  200.8 1.9 collective-permute-start.3
  202.8 1.9 collective-permute-start.4
  204.7 5.0 %fusion.3 = f32[2048,576]{0,1:T(8,128)} fusion(bf16[384,576]{1,0:T(8,128)(2,1)S(1)} %bitcast.13, bf16[768,2048]{1,0:T(8,128)(2,1)} %copy-done.4, s32[]{:T(128)S(6)} %select_n.14), kind=kOutput, calls=%fused_computation.2 | convolution fusion | flops 905969664 | bytes 6733828 | tf_op jit(solution)/shard_map/dot_general | solution.py:46
  209.7 2.5 %collective-permute-done.4 = f32[12,2304]{1,0:T(8,128)S(1)} collective-permute-done((f32[12,2304]{1,0:T(8,128)S(1)}, f32[12,2304]{1,0:T(8,128)S(1)}, u32[]{:S(2)}, u32[]{:S(2)}) %collective-permute-start.4) | collective-permute-done | bytes 110624
  212.2 0.0 collective-permute-done.3
  212.3 0.4 concatenate.7
  212.6 0.7 constant_dynamic-slice_fusion
  (9 shorter events, 0.1 us)
Async XLA Ops:
  7.2 14.7 %copy-start = (bf16[2048,576]{0,1:T(8,128)(2,1)S(1)}, bf16[2048,576]{0,1:T(8,128)(2,1)}, u32[]{:S(2)}) copy-start(bf16[2048,576]{0,1:T(8,128)(2,1)} %param.4) | copy-start | bytes 7077892
  7.2 62.7 %reduce-scatter.4.cloned.1.call-start = ((), (), s32[]{:S(2)}) async-start(), calls=%async_computation.3 | async-start | bytes 3932160 | tf_op jit(solution)/shard_map/reduce_scatter | solution.py:12
  21.8 3.1 %copy-start.1 = (bf16[96,2048]{1,0:T(8,128)(2,1)S(1)}, bf16[96,2048]{1,0:T(8,128)(2,1)}, u32[]{:S(2)}) copy-start(bf16[96,2048]{1,0:T(8,128)(2,1)} %param.5) | copy-start | bytes 1179652
  105.8 12.0 %collective-permute-start = (bf16[96,2048]{1,0:T(8,128)(2,1)S(1)}, bf16[96,2048]{1,0:T(8,128)(2,1)S(1)}, u32[]{:S(2)}, u32[]{:S(2)}) collective-permute-start(bf16[96,2048]{1,0:T(8,128)(2,1)S(1)} %fusion.10), channel_id=1, source_target_pairs={{0,8},{8,16},{16,24},{24,0},{1,9},{9,17},{17,25},{25,1},{2,10},{10... | collective-permute-start | bytes 1179656 | tf_op jit(solution)/shard_map/ppermute | solution.py:38
  117.7 0.7 copy-start.2
  118.5 11.2 %collective-permute-start.1 = (bf16[96,2048]{1,0:T(8,128)(2,1)S(1)}, bf16[96,2048]{1,0:T(8,128)(2,1)}, u32[]{:S(2)}, u32[]{:S(2)}) collective-permute-start(bf16[96,2048]{1,0:T(8,128)(2,1)S(1)} %collective-permute-done), channel_id=1, source_target_pairs={{0,8},{8,16},{16,24},{24,0},{1,9},{9,17},{17,25},{25,1},{2,10},{10... | collective-permute-start | bytes 1179656 | tf_op jit(solution)/shard_map/ppermute | solution.py:38
  129.6 10.5 %collective-permute-start.2 = (bf16[96,2048]{1,0:T(8,128)(2,1)}, bf16[96,2048]{1,0:T(8,128)(2,1)}, u32[]{:S(2)}, u32[]{:S(2)}) collective-permute-start(bf16[96,2048]{1,0:T(8,128)(2,1)} %collective-permute-done.1), channel_id=1, source_target_pairs={{0,8},{8,16},{16,24},{24,0},{1,9},{9,17},{17,25},{25,1},{2,10},{10... | collective-permute-start | bytes 1179656 | tf_op jit(solution)/shard_map/ppermute | solution.py:38
  129.6 15.7 %copy-start.3 = (bf16[96,2048]{1,0:T(8,128)(2,1)S(1)}, bf16[96,2048]{1,0:T(8,128)(2,1)}, u32[]{:S(2)}) copy-start(bf16[96,2048]{1,0:T(8,128)(2,1)} %copy-done.2) | copy-start | bytes 1179652
  145.4 2.4 %copy-start.4 = (bf16[768,2048]{1,0:T(8,128)(2,1)}, bf16[768,2048]{1,0:T(8,128)(2,1)S(1)}, u32[]{:S(2)}) copy-start(bf16[768,2048]{1,0:T(8,128)(2,1)S(1)} %constant_dynamic-update-slice_fusion) | copy-start | bytes 9437188
  145.4 6.6 %copy-start.5 = (u32[32]{0:T(128)S(1)}, u32[32]{0:T(128)}, u32[]{:S(2)}) copy-start(u32[32]{0:T(128)} %constant.38) | copy-start | bytes 388
  147.8 16.8 %all-to-all-start.1 = ((f32[4,96,576]{2,1,0:T(8,128)}), f32[4,96,576]{2,1,0:T(8,128)}, u32[]{:S(2)}, u32[]{:S(2)}) async-start(f32[4,96,576]{2,1,0:T(8,128)} %bitcast.14), calls=%async_computation.2 | async-start | bytes 1966080 | tf_op jit(solution)/shard_map/all_to_all | solution.py:50
  200.8 11.4 %collective-permute-start.3 = (f32[16,2304]{1,0:T(8,128)S(1)}, f32[16,2304]{1,0:T(8,128)S(1)}, u32[]{:S(2)}, u32[]{:S(2)}) collective-permute-start(f32[16,2304]{1,0:T(8,128)S(1)} %fusion), channel_id=1, source_target_pairs={{0,1},{1,2},{2,3},{3,4},{4,5},{5,6},{6,7},{8,9},{9,10},{10,11},{11... | collective-permute-start | bytes 442376
  202.8 9.5 %collective-permute-start.4 = (f32[12,2304]{1,0:T(8,128)S(1)}, f32[12,2304]{1,0:T(8,128)S(1)}, u32[]{:S(2)}, u32[]{:S(2)}) collective-permute-start(f32[12,2304]{1,0:T(8,128)S(1)} %slice), channel_id=1, source_target_pairs={{0,2},{1,3},{2,4},{3,5},{4,6},{5,7},{8,10},{9,11},{10,12},{11,13},... | collective-permute-start | bytes 331784
Sparse Core Ops, SparseCore 0:
  25.0 44.7 reduce-scatter.3
